TPU v7x, 8 devices: a whole 2x2x1 slice. The times are simulated.
8 devices in a mesh: pod: 1 (over z), dp: 2 (over y), ep: 4 (over x, core).
Axes of the slice: x: 2, y: 2, z: 1, core: 2. Of those that a mesh axis runs over, the one named last changes fastest.
Arguments:
- x_start: bfloat16 [8192, 1024], P(('pod', 'dp', 'ep'))
- route_a: int32 [8192, 2], P(('pod', 'dp', 'ep'))
- route_b: int32 [8192, 2], P(('pod', 'dp', 'ep'))
- gate_a: float32 [8192, 2], P(('pod', 'dp', 'ep'))
- gate_b: float32 [8192, 2], P(('pod', 'dp', 'ep'))
- grad_out: bfloat16 [8192, 1024], P(('pod', 'dp', 'ep'))
- w1_a: bfloat16 [8, 1024, 3584], P('ep')
- w3_a: bfloat16 [8, 1024, 3584], P('ep')
- w2_a: bfloat16 [8, 3584, 1024], P('ep')
- w1_b: bfloat16 [8, 1024, 3584], P('ep')
- w3_b: bfloat16 [8, 1024, 3584], P('ep')
- w2_b: bfloat16 [8, 3584, 1024], P('ep')
Outputs:
- output 1: bfloat16 [8192, 1024], P(('pod', 'dp', 'ep'))
- output 2: bfloat16 [8192, 1024], P(('pod', 'dp', 'ep'))
- output 3: float32 [8, 1024, 3584], P(('pod', 'ep'), 'dp')
- output 4: float32 [8, 1024, 3584], P(('pod', 'ep'), 'dp')
- output 5: float32 [8, 3584, 1024], P(('pod', 'ep'), 'dp')
- output 6: float32 [8, 1024, 3584], P(('pod', 'ep'), 'dp')
- output 7: float32 [8, 1024, 3584], P(('pod', 'ep'), 'dp')
- output 8: float32 [8, 3584, 1024], P(('pod', 'ep'), 'dp')
- output 9: float32 [8192, 2], P(('pod', 'dp', 'ep'))
- output 10: float32 [8192, 2], P(('pod', 'dp', 'ep'))
All inputs are finite; a program needn't handle non-finite values.
Results may differ from a plain program's by a relative error of at most 0.00888651.
Values are sent between devices in bfloat16 or wider.
A program may use at most 1 GiB of HBM per device.

v0:
```python
import jax
import jax.numpy as jnp
from jax import lax
from jax.sharding import PartitionSpec as P


def route_rows(expert_ids, n_experts, capacity):
    n_tokens, top_k = expert_ids.shape
    flat_ids = expert_ids.reshape(-1)
    onehot = (flat_ids[:, None] == jnp.arange(n_experts, dtype=jnp.int32)[None, :]).astype(jnp.int32)
    earlier = jnp.cumsum(onehot, axis=0) - onehot
    slot_idx = jnp.sum(earlier * onehot, axis=1)
    pair_row = flat_ids * capacity + slot_idx
    pair_tok = jnp.arange(n_tokens * top_k, dtype=jnp.int32) // top_k
    row_tok = jnp.zeros((n_experts * capacity,), jnp.int32).at[pair_row].set(pair_tok)
    row_used = jnp.zeros((n_experts * capacity,), jnp.bfloat16).at[pair_row].set(1.0)
    return pair_row, row_tok, row_used


def take_rows(values, row_tok, row_used):
    return jnp.take(values, row_tok, axis=0) * row_used[:, None]


def place_gates(gate_vals, pair_row, n_rows):
    return jnp.zeros((n_rows,), jnp.float32).at[pair_row].set(gate_vals.reshape(-1))


def mix_back(x_in, out_rows, pair_row, gate_vals):
    n_tokens, top_k = gate_vals.shape
    pair_out = jnp.take(out_rows, pair_row, axis=0).reshape(n_tokens, top_k, -1)
    mixed_sum = jnp.sum(gate_vals[:, :, None] * pair_out, axis=1)
    return (x_in.astype(jnp.float32) + mixed_sum).astype(jnp.bfloat16)


def add_back(grad_in, du_rows, pair_row, gate_grad_rows, top_k):
    n_tokens = grad_in.shape[0]
    pair_grad = jnp.take(du_rows, pair_row, axis=0).reshape(n_tokens, top_k, -1)
    grad_x = (grad_in.astype(jnp.float32) + jnp.sum(pair_grad, axis=1, dtype=jnp.float32)).astype(jnp.bfloat16)
    return grad_x, jnp.take(gate_grad_rows, pair_row, axis=0).reshape(n_tokens, top_k)


def expert_forward(recv_rows, w_up1, w_up3, w_down):
    pre_one = jnp.einsum('secd,edf->escf', recv_rows, w_up1, preferred_element_type=jnp.float32)
    pre_three = jnp.einsum('secd,edf->escf', recv_rows, w_up3, preferred_element_type=jnp.float32)
    hidden = (jax.nn.silu(pre_one) * pre_three).astype(jnp.bfloat16)
    return jnp.einsum('escf,efd->secd', hidden, w_down, preferred_element_type=jnp.float32).astype(jnp.bfloat16)


def expert_backward(recv_rows, recv_dy, recv_gate, w_up1, w_up3, w_down):
    pre_one = jnp.einsum('secd,edf->escf', recv_rows, w_up1, preferred_element_type=jnp.float32)
    pre_three = jnp.einsum('secd,edf->escf', recv_rows, w_up3, preferred_element_type=jnp.float32)
    sig_one = jax.nn.sigmoid(pre_one)
    act_one = pre_one * sig_one
    hidden = (act_one * pre_three).astype(jnp.bfloat16)
    back_proj = jnp.einsum('secd,efd->escf', recv_dy, w_down, preferred_element_type=jnp.float32)
    gate_grad = jnp.sum(back_proj * hidden, axis=-1)
    gate_esc = jnp.transpose(recv_gate, (1, 0, 2))
    scaled_dy = (recv_gate[..., None] * recv_dy).astype(jnp.bfloat16)
    dw_down = jnp.einsum('escf,secd->efd', hidden, scaled_dy, preferred_element_type=jnp.float32)
    d_hidden = gate_esc[..., None] * back_proj
    d_pre_one = (d_hidden * pre_three * sig_one * (1.0 + pre_one * (1.0 - sig_one))).astype(jnp.bfloat16)
    d_pre_three = (d_hidden * act_one).astype(jnp.bfloat16)
    dw_up1 = jnp.einsum('secd,escf->edf', recv_rows, d_pre_one, preferred_element_type=jnp.float32)
    dw_up3 = jnp.einsum('secd,escf->edf', recv_rows, d_pre_three, preferred_element_type=jnp.float32)
    grad_rows = (jnp.einsum('escf,edf->secd', d_pre_one, w_up1, preferred_element_type=jnp.float32)
                 + jnp.einsum('escf,edf->secd', d_pre_three, w_up3, preferred_element_type=jnp.float32)).astype(jnp.bfloat16)
    return grad_rows, jnp.transpose(gate_grad, (1, 0, 2)), dw_up1, dw_up3, dw_down


def solution(mesh):
    n_ep = mesh.shape['ep']
    tok_spec = P(('pod', 'dp', 'ep'), None)
    weight_spec = P('ep', None, None)
    grad_spec = P(('pod', 'ep'), 'dp', None)

    def local_step(x_start, route_a, route_b, gate_a, gate_b, grad_out, w1_a, w3_a, w2_a, w1_b, w3_b, w2_b):
        n_tokens = x_start.shape[0]
        top_k = route_a.shape[1]
        n_local = w1_a.shape[0]
        n_experts = n_local * n_ep
        capacity = 3 * n_tokens * top_k // (2 * n_experts)
        n_rows = n_experts * capacity

        def exchange(send_rows):
            shaped = send_rows.reshape((n_ep, n_local, capacity) + send_rows.shape[1:])
            return lax.all_to_all(shaped, 'ep', 0, 0)

        def give_back(expert_rows):
            returned = lax.all_to_all(expert_rows, 'ep', 0, 0)
            return returned.reshape((n_rows,) + expert_rows.shape[3:])

        def layer_backward(recv_rows, grad_in, route_plan, gate_vals, w_up1, w_up3, w_down):
            pair_row, row_tok, row_used = route_plan
            recv_dy = exchange(take_rows(grad_in, row_tok, row_used))
            recv_gate = exchange(place_gates(gate_vals, pair_row, n_rows))
            grad_rows, gate_grad, dw_up1, dw_up3, dw_down = expert_backward(recv_rows, recv_dy, recv_gate, w_up1, w_up3, w_down)
            grad_x, gate_out = add_back(grad_in, give_back(grad_rows), pair_row, give_back(gate_grad), top_k)
            dw_parts = [lax.psum_scatter(grad_part, 'dp', scatter_dimension=1, tiled=True) for grad_part in (dw_up1, dw_up3, dw_down)]
            return grad_x, gate_out, dw_parts[0], dw_parts[1], dw_parts[2]

        plan_a = route_rows(route_a, n_experts, capacity)
        plan_b = route_rows(route_b, n_experts, capacity)
        recv_a = exchange(take_rows(x_start, plan_a[1], plan_a[2]))
        x_mid = mix_back(x_start, give_back(expert_forward(recv_a, w1_a, w3_a, w2_a)), plan_a[0], gate_a)
        recv_b = exchange(take_rows(x_mid, plan_b[1], plan_b[2]))
        x_final = mix_back(x_mid, give_back(expert_forward(recv_b, w1_b, w3_b, w2_b)), plan_b[0], gate_b)
        x_kept, recv_b_kept, grad_kept = lax.optimization_barrier((x_start, recv_b, grad_out))
        grad_mid, dgate_b, dw1_b, dw3_b, dw2_b = layer_backward(recv_b_kept, grad_kept, plan_b, gate_b, w1_b, w3_b, w2_b)
        recv_a_again = exchange(take_rows(x_kept, plan_a[1], plan_a[2]))
        grad_x, dgate_a, dw1_a, dw3_a, dw2_a = layer_backward(recv_a_again, grad_mid, plan_a, gate_a, w1_a, w3_a, w2_a)
        return (x_final, grad_x, dw1_a, dw3_a, dw2_a, dw1_b, dw3_b, dw2_b, dgate_a, dgate_b)

    return jax.shard_map(local_step, mesh=mesh,
                         in_specs=(tok_spec,) * 6 + (weight_spec,) * 6,
                         out_specs=(tok_spec, tok_spec) + (grad_spec,) * 6 + (tok_spec, tok_spec),
                         check_vma=False)
```

profile of v0, /device:TPU:0, one launch (start us, length us, event | category | flops | bytes accessed | tf_op | source)
XLA Modules:
  0.0 2603.4 jit_solution(16793010702155467083)
XLA Ops:
  53.7 75.5 %all_to_all.65 = bf16[4,2,384,1024]{3,2,1,0:T(8,128)(2,1)S(1)} all-to-all(bf16[4,2,384,1024]{3,2,1,0:T(8,128)(2,1)S(1)} %bitcast.177), channel_id=1, replica_groups=mesh['pod'=1,'dp'=2,'ep'=4] {'ep'}, dimensions={0} | all-to-all | bytes 12582912 | tf_op jit(solution)/shard_map/all_to_all | solution.py:86
  161.8 38.1 %multiply_convert_fusion.25 = bf16[2,4,384,3584]{3,2,1,0:T(8,128)(2,1)} fusion(f32[2,4,384,3584]{3,2,1,0:T(8,128)} %fusion.26, bf16[2,1024,3584]{2,1,0:T(8,128)(2,1)} %param.24, bf16[4,2,384,1024]{3,2,1,0:T(8,128)(2,1)} %copy-done.8), kind=kOutput, calls=%fused_computation.30.clone.clone.clone.clone | convolution fusion | flops 22614638592 | bytes 87031808 | tf_op jit(solution)/shard_map/secd,edf->escf/dot_general | solution.py:43
  199.9 31.3 %convert_bitcast_fusion.1 = bf16[4,2,384,1024]{3,2,0,1:T(8,128)(2,1)} fusion(bf16[2,3584,1024]{2,1,0:T(8,128)(2,1)} %param.26, bf16[2,4,384,3584]{3,2,1,0:T(8,128)(2,1)} %multiply_convert_fusion.25), kind=kOutput, calls=%fused_computation.95 | convolution fusion | flops 22551724032 | bytes 42991616 | tf_op jit(solution)/shard_map/escf,efd->secd/dot_general | solution.py:46
  279.9 33.5 %all-to-all-done.1 = bf16[4,2,384,1024]{3,2,1,0:T(8,128)(2,1)} async-done(((bf16[4,2,384,1024]{3,2,1,0:T(8,128)(2,1)}), bf16[4,2,384,1024]{3,2,1,0:T(8,128)(2,1)}, u32[]{:S(2)}, u32[]{:S(2)}) %all-to-all-start.1) | async-done | bytes 6291488 | tf_op jit(solution)/shard_map/all_to_all | solution.py:89
  386.3 70.3 %all-to-all-done.2 = bf16[4,2,384,1024]{3,2,1,0:T(8,128)(2,1)} async-done(((bf16[4,2,384,1024]{3,2,1,0:T(8,128)(2,1)}), bf16[4,2,384,1024]{3,2,1,0:T(8,128)(2,1)}, u32[]{:S(2)}, u32[]{:S(2)}) %all-to-all-start.2) | async-done | bytes 6291488 | tf_op jit(solution)/shard_map/all_to_all | solution.py:86
  482.7 33.8 %fusion.33 = f32[2,4,384,3584]{3,2,1,0:T(8,128)} fusion(bf16[2,1024,3584]{2,1,0:T(8,128)(2,1)} %param.27, bf16[4,2,384,1024]{3,2,1,0:T(8,128)(2,1)} %all-to-all-done.2), kind=kOutput, calls=%fused_computation.58 | convolution fusion | flops 22548578304 | bytes 65011712 | tf_op jit(solution)/shard_map/secd,edf->escf/dot_general | solution.py:50
  516.4 33.3 %fusion.43 = f32[2,4,384,3584]{3,2,1,0:T(8,128)} fusion(bf16[2,1024,3584]{2,1,0:T(8,128)(2,1)} %param.28, bf16[4,2,384,1024]{3,2,1,0:T(8,128)(2,1)} %all-to-all-done.2), kind=kOutput, calls=%fused_computation.64 | convolution fusion | flops 22548578304 | bytes 65011712 | tf_op jit(solution)/shard_map/secd,edf->escf/dot_general | solution.py:51
  553.0 69.1 %multiply_reduce_fusion = (f32[2,4,384]{2,1,0:T(4,128)}, bf16[2,4,384,3584]{3,2,1,0:T(8,128)(2,1)}, bf16[2,4,384,3584]{3,2,1,0:T(8,128)(2,1)}, bf16[2,4,384,3584]{3,2,1,0:T(8,128)(2,1)}) fusion(f32[2,4,384,3584]{3,2,1,0:T(8,128)} %fusion.43, f32[2,4,384,3584]{3,2,1,0:T(8,128)} %fusion.33, f32[2,4,384]{2,1,0:T(4,128)S(1)} %copy.114, ...), kind=kOutput, calls=%fused_computation.17 | convolution fusion | flops 22757765120 | bytes 175136768 | tf_op jit(solution)/shard_map/secd,efd->escf/dot_general | solution.py:55
  652.7 30.8 %fusion.56 = f32[2,1024,3584]{2,1,0:T(8,128)} fusion(bf16[4,2,384,1024]{3,2,1,0:T(8,128)(2,1)} %all-to-all-done.2, bf16[2,4,384,3584]{3,2,1,0:T(8,128)(2,1)} %get-tuple-element.56), kind=kOutput, calls=%fused_computation.73 | convolution fusion | flops 22548578304 | bytes 57671680 | tf_op jit(solution)/shard_map/secd,escf->edf/dot_general | solution.py:63
  683.6 33.3 %fusion.45 = f32[2,4,384,3584]{3,2,1,0:T(8,128)} fusion(bf16[2,1024,3584]{2,1,0:T(8,128)(2,1)} %param.28, bf16[4,2,384,1024]{3,2,1,0:T(8,128)(2,1)} %all-to-all-done.2), kind=kOutput, calls=%fused_computation.66 | convolution fusion | flops 22548578304 | bytes 65011712 | tf_op jit(solution)/shard_map/secd,edf->escf/dot_general | solution.py:44
  717.0 38.1 %multiply_convert_fusion.24 = bf16[2,4,384,3584]{3,2,1,0:T(8,128)(2,1)} fusion(f32[2,4,384,3584]{3,2,1,0:T(8,128)} %fusion.45, bf16[2,1024,3584]{2,1,0:T(8,128)(2,1)} %param.27, bf16[4,2,384,1024]{3,2,1,0:T(8,128)(2,1)} %all-to-all-done.2), kind=kOutput, calls=%fused_computation.29.clone.clone.clone.clone.1 | convolution fusion | flops 22614638592 | bytes 87031808 | tf_op jit(solution)/shard_map/secd,edf->escf/dot_general | solution.py:43
  755.0 32.2 %convolution_bitcast_fusion = f32[2,3584,1024]{2,1,0:T(8,128)} fusion(bf16[2,4,384,3584]{3,2,1,0:T(8,128)(2,1)} %get-tuple-element.52, bf16[4,2,384,1024]{3,2,1,0:T(8,128)(2,1)} %all-to-all-done.5, f32[4,2,384]{2,1,0:T(2,128)S(1)} %copy-done.30), kind=kOutput, calls=%fused_computation.75 | convolution fusion | flops 22558015488 | bytes 57683968 | tf_op jit(solution)/shard_map/escf,secd->efd/dot_general | solution.py:59
  787.3 31.4 %convert_bitcast_fusion = bf16[4,2,384,1024]{3,2,0,1:T(8,128)(2,1)} fusion(bf16[2,3584,1024]{2,1,0:T(8,128)(2,1)} %param.29, bf16[2,4,384,3584]{3,2,1,0:T(8,128)(2,1)} %multiply_convert_fusion.24), kind=kOutput, calls=%fused_computation.94 | convolution fusion | flops 22551724032 | bytes 42991616 | tf_op jit(solution)/shard_map/escf,efd->secd/dot_general | solution.py:46
  861.0 39.8 %all-to-all-done.3 = bf16[4,2,384,1024]{3,2,1,0:T(8,128)(2,1)} async-done(((bf16[4,2,384,1024]{3,2,1,0:T(8,128)(2,1)}), bf16[4,2,384,1024]{3,2,1,0:T(8,128)(2,1)}, u32[]{:S(2)}, u32[]{:S(2)}) %all-to-all-start.3) | async-done | bytes 6291488 | tf_op jit(solution)/shard_map/all_to_all | solution.py:89
  1100.4 70.3 %all-to-all-done.9 = bf16[4,2,384,1024]{3,2,1,0:T(8,128)(2,1)} async-done(((bf16[4,2,384,1024]{3,2,1,0:T(8,128)(2,1)}), bf16[4,2,384,1024]{3,2,1,0:T(8,128)(2,1)}, u32[]{:S(2)}, u32[]{:S(2)}) %all-to-all-start.9) | async-done | bytes 6291488 | tf_op jit(solution)/shard_map/all_to_all | solution.py:86
  1176.1 33.8 %fusion.14 = f32[2,4,384,3584]{3,2,1,0:T(8,128)} fusion(bf16[2,1024,3584]{2,1,0:T(8,128)(2,1)} %param.24, bf16[4,2,384,1024]{3,2,1,0:T(8,128)(2,1)} %all-to-all-done.9), kind=kOutput, calls=%fused_computation.43 | convolution fusion | flops 22548578304 | bytes 65011712 | tf_op jit(solution)/shard_map/secd,edf->escf/dot_general | solution.py:50
  1209.8 33.3 %fusion.24 = f32[2,4,384,3584]{3,2,1,0:T(8,128)} fusion(bf16[2,1024,3584]{2,1,0:T(8,128)(2,1)} %param.25, bf16[4,2,384,1024]{3,2,1,0:T(8,128)(2,1)} %all-to-all-done.9), kind=kOutput, calls=%fused_computation.49 | convolution fusion | flops 22548578304 | bytes 65011712 | tf_op jit(solution)/shard_map/secd,edf->escf/dot_general | solution.py:51
  1246.4 69.1 %multiply_reduce_fusion.1 = (f32[2,4,384]{2,1,0:T(4,128)}, bf16[2,4,384,3584]{3,2,1,0:T(8,128)(2,1)}, bf16[2,4,384,3584]{3,2,1,0:T(8,128)(2,1)}, bf16[2,4,384,3584]{3,2,1,0:T(8,128)(2,1)}) fusion(f32[2,4,384,3584]{3,2,1,0:T(8,128)} %fusion.24, f32[2,4,384,3584]{3,2,1,0:T(8,128)} %fusion.14, f32[2,4,384]{2,1,0:T(4,128)S(1)} %copy.120, ...), kind=kOutput, calls=%fused_computation.18 | convolution fusion | flops 22757765120 | bytes 175136768 | tf_op jit(solution)/shard_map/secd,efd->escf/dot_general | solution.py:55
  1346.2 30.9 %fusion.50 = f32[2,1024,3584]{2,1,0:T(8,128)} fusion(bf16[4,2,384,1024]{3,2,1,0:T(8,128)(2,1)} %all-to-all-done.9, bf16[2,4,384,3584]{3,2,1,0:T(8,128)(2,1)} %get-tuple-element.55), kind=kOutput, calls=%fused_computation.71 | convolution fusion | flops 22548578304 | bytes 57671680 | tf_op jit(solution)/shard_map/secd,escf->edf/dot_general | solution.py:63
  1377.8 32.1 %convolution_bitcast_fusion.1 = f32[2,3584,1024]{2,1,0:T(8,128)} fusion(bf16[2,4,384,3584]{3,2,1,0:T(8,128)(2,1)} %get-tuple-element.54, bf16[4,2,384,1024]{3,2,1,0:T(8,128)(2,1)} %all-to-all-done.8, f32[4,2,384]{2,1,0:T(2,128)S(1)} %copy-done.28), kind=kOutput, calls=%fused_computation.76 | convolution fusion | flops 22558015488 | bytes 57683968 | tf_op jit(solution)/shard_map/escf,secd->efd/dot_general | solution.py:59
  1526.3 31.1 %all-to-all-done.10 = bf16[4,2,384,1024]{3,2,1,0:T(8,128)(2,1)} async-done(((bf16[4,2,384,1024]{3,2,1,0:T(8,128)(2,1)}), bf16[4,2,384,1024]{3,2,1,0:T(8,128)(2,1)}, u32[]{:S(2)}, u32[]{:S(2)}) %all-to-all-start.10) | async-done | bytes 6291488 | tf_op jit(solution)/shard_map/all_to_all | solution.py:89
  1623.5 324.3 %reduce-scatter.9.cloned.1.call-done = f32[2,512,3584]{2,1,0:T(8,128)} async-done(((f32[2,1024,3584]{2,1,0:T(8,128)}), f32[2,512,3584]{2,1,0:T(8,128)}) %reduce-scatter.9.cloned.1.call-update) | async-done | bytes 14680080 | tf_op jit(solution)/shard_map/reduce_scatter | solution.py:98
  1947.8 324.3 %reduce-scatter.7.cloned.1.call-done = f32[2,512,3584]{2,1,0:T(8,128)} async-done(((f32[2,1024,3584]{2,1,0:T(8,128)}), f32[2,512,3584]{2,1,0:T(8,128)}) %reduce-scatter.7.cloned.1.call-update) | async-done | bytes 14680080 | tf_op jit(solution)/shard_map/reduce_scatter | solution.py:98
  2272.1 324.3 %reduce-scatter.11.cloned.1.call-done = f32[2,1792,1024]{2,1,0:T(8,128)} async-done(((f32[2,3584,1024]{2,1,0:T(8,128)}), f32[2,1792,1024]{2,1,0:T(8,128)}) %reduce-scatter.11.cloned.1.call-update) | async-done | bytes 14680080 | tf_op jit(solution)/shard_map/reduce_scatter | solution.py:98
  (222 shorter events, 724.3 us)
Async XLA Ops:
  237.4 76.0 %all-to-all-start.1 = ((bf16[4,2,384,1024]{3,2,1,0:T(8,128)(2,1)}), bf16[4,2,384,1024]{3,2,1,0:T(8,128)(2,1)}, u32[]{:S(2)}, u32[]{:S(2)}) async-start(bf16[4,2,384,1024]{3,2,1,0:T(8,128)(2,1)} %copy.105), calls=%async_computation.1 | async-start | bytes 12582912 | tf_op jit(solution)/shard_map/all_to_all | solution.py:89
  270.6 76.7 %copy-start.11 = (f32[1024,2]{1,0:T(8,128)}, f32[1024,2]{1,0:T(8,128)S(1)}, u32[]{:S(2)}) copy-start(f32[1024,2]{1,0:T(8,128)S(1)} %copy.99) | copy-start | bytes 24580
  270.8 60.6 %copy-start.9 = (f32[1024,2]{1,0:T(8,128)}, f32[1024,2]{1,0:T(8,128)S(1)}, u32[]{:S(2)}) copy-start(f32[1024,2]{1,0:T(8,128)S(1)} %copy.106) | copy-start | bytes 24580
  279.8 51.6 %copy-start.33 = (pred[2048]{0:T(1024)(128)(4,1)}, pred[2048]{0:T(1024)(128)(4,1)S(1)}, u32[]{:S(2)}) copy-start(pred[2048]{0:T(1024)(128)(4,1)S(1)} %compare_and_fusion.3) | copy-start | bytes 6148
  313.4 67.5 %all-to-all-start.4 = ((f32[4,2,384]{2,1,0:T(2,128)}), f32[4,2,384]{2,1,0:T(2,128)S(1)}, u32[]{:S(2)}, u32[]{:S(2)}) async-start(f32[4,2,384]{2,1,0:T(2,128)} %reshape.205), calls=%async_computation.4 | async-start | bytes 24576 | tf_op jit(solution)/shard_map/all_to_all | solution.py:86
  380.9 75.8 %copy-start.7 = (bf16[1024,1024]{1,0:T(8,128)(2,1)S(1)}, bf16[1024,1024]{1,0:T(8,128)(2,1)}, u32[]{:S(2)}) copy-start(bf16[1024,1024]{1,0:T(8,128)(2,1)} %param.23) | copy-start | bytes 6291460
  380.9 89.7 %copy-start.29 = (f32[4,2,384]{2,1,0:T(2,128)}, f32[4,2,384]{2,1,0:T(2,128)S(1)}, u32[]{:S(2)}) copy-start(f32[4,2,384]{2,1,0:T(2,128)S(1)} %all-to-all-done.4) | copy-start | bytes 36868
  380.9 75.8 %all-to-all-start.2 = ((bf16[4,2,384,1024]{3,2,1,0:T(8,128)(2,1)}), bf16[4,2,384,1024]{3,2,1,0:T(8,128)(2,1)}, u32[]{:S(2)}, u32[]{:S(2)}) async-start(bf16[4,2,384,1024]{3,2,1,0:T(8,128)(2,1)} %bitcast.175), calls=%async_computation.2 | async-start | bytes 12582912 | tf_op jit(solution)/shard_map/all_to_all | solution.py:86
  477.4 75.6 %all-to-all-start.5 = ((bf16[4,2,384,1024]{3,2,1,0:T(8,128)(2,1)}), bf16[4,2,384,1024]{3,2,1,0:T(8,128)(2,1)}, u32[]{:S(2)}, u32[]{:S(2)}) async-start(bf16[4,2,384,1024]{3,2,1,0:T(8,128)(2,1)} %bitcast.176), calls=%async_computation.5 | async-start | bytes 12582912 | tf_op jit(solution)/shard_map/all_to_all | solution.py:86
  482.6 1122.4 %reduce-scatter.15.cloned.1.call-start = ((), (), s32[]{:S(2)}) async-start(), calls=%async_computation.23 | async-start | bytes 44040192 | tf_op jit(solution)/shard_map/reduce_scatter | solution.py:98
  652.7 952.4 %reduce-scatter.13.cloned.1.call-start = ((), (), s32[]{:S(2)}) async-start(), calls=%async_computation.22 | async-start | bytes 44040192 | tf_op jit(solution)/shard_map/reduce_scatter | solution.py:98
  683.6 939.9 %reduce-scatter.17.cloned.1.call-start = ((), (), s32[]{:S(2)}) async-start(), calls=%async_computation.24 | async-start | bytes 44040192 | tf_op jit(solution)/shard_map/reduce_scatter | solution.py:98
  824.8 76.0 %all-to-all-start.3 = ((bf16[4,2,384,1024]{3,2,1,0:T(8,128)(2,1)}), bf16[4,2,384,1024]{3,2,1,0:T(8,128)(2,1)}, u32[]{:S(2)}, u32[]{:S(2)}) async-start(bf16[4,2,384,1024]{3,2,1,0:T(8,128)(2,1)} %copy.112), calls=%async_computation.3 | async-start | bytes 12582912 | tf_op jit(solution)/shard_map/all_to_all | solution.py:89
  900.8 40.1 %all-to-all-start.12 = ((f32[4,2,384]{2,1,0:T(2,128)}), f32[4,2,384]{2,1,0:T(2,128)S(1)}, u32[]{:S(2)}, u32[]{:S(2)}) async-start(f32[4,2,384]{2,1,0:T(2,128)} %copy.138), calls=%async_computation.18 | async-start | bytes 24576 | tf_op jit(solution)/shard_map/all_to_all | solution.py:89
  940.9 75.9 %all-to-all-start.6 = ((bf16[4,2,384,1024]{3,2,1,0:T(8,128)(2,1)}), bf16[4,2,384,1024]{3,2,1,0:T(8,128)(2,1)}, u32[]{:S(2)}, u32[]{:S(2)}) async-start(bf16[4,2,384,1024]{3,2,1,0:T(8,128)(2,1)} %copy.118), calls=%async_computation.6 | async-start | bytes 12582912 | tf_op jit(solution)/shard_map/all_to_all | solution.py:89
  1016.8 78.3 %all-to-all-start.7 = ((f32[4,2,384]{2,1,0:T(2,128)}), f32[4,2,384]{2,1,0:T(2,128)S(1)}, u32[]{:S(2)}, u32[]{:S(2)}) async-start(f32[4,2,384]{2,1,0:T(2,128)} %reshape.209), calls=%async_computation.7 | async-start | bytes 24576 | tf_op jit(solution)/shard_map/all_to_all | solution.py:86
  1095.1 75.6 %copy-start.27 = (f32[4,2,384]{2,1,0:T(2,128)}, f32[4,2,384]{2,1,0:T(2,128)S(1)}, u32[]{:S(2)}) copy-start(f32[4,2,384]{2,1,0:T(2,128)S(1)} %all-to-all-done.7) | copy-start | bytes 36868
  1095.1 75.6 %all-to-all-start.9 = ((bf16[4,2,384,1024]{3,2,1,0:T(8,128)(2,1)}), bf16[4,2,384,1024]{3,2,1,0:T(8,128)(2,1)}, u32[]{:S(2)}, u32[]{:S(2)}) async-start(bf16[4,2,384,1024]{3,2,1,0:T(8,128)(2,1)} %bitcast.179), calls=%async_computation.9 | async-start | bytes 12582912 | tf_op jit(solution)/shard_map/all_to_all | solution.py:86
  1170.7 75.6 %all-to-all-start.8 = ((bf16[4,2,384,1024]{3,2,1,0:T(8,128)(2,1)}), bf16[4,2,384,1024]{3,2,1,0:T(8,128)(2,1)}, u32[]{:S(2)}, u32[]{:S(2)}) async-start(bf16[4,2,384,1024]{3,2,1,0:T(8,128)(2,1)} %bitcast.178), calls=%async_computation.8 | async-start | bytes 12582912 | tf_op jit(solution)/shard_map/all_to_all | solution.py:86
  1176.0 771.8 %reduce-scatter.9.cloned.1.call-start = ((), (), s32[]{:S(2)}) async-start(), calls=%async_computation.20 | async-start | bytes 44040192 | tf_op jit(solution)/shard_map/reduce_scatter | solution.py:98
  1346.1 925.9 %reduce-scatter.7.cloned.1.call-start = ((), (), s32[]{:S(2)}) async-start(), calls=%async_computation.19 | async-start | bytes 44040192 | tf_op jit(solution)/shard_map/reduce_scatter | solution.py:98
  1377.1 1219.3 %reduce-scatter.11.cloned.1.call-start = ((), (), s32[]{:S(2)}) async-start(), calls=%async_computation.21 | async-start | bytes 44040192 | tf_op jit(solution)/shard_map/reduce_scatter | solution.py:98
  1411.2 70.4 %all-to-all-start.11 = ((f32[4,2,384]{2,1,0:T(2,128)}), f32[4,2,384]{2,1,0:T(2,128)S(1)}, u32[]{:S(2)}, u32[]{:S(2)}) async-start(f32[4,2,384]{2,1,0:T(2,128)} %copy.137), calls=%async_computation.17 | async-start | bytes 24576 | tf_op jit(solution)/shard_map/all_to_all | solution.py:89
  1481.5 75.9 %all-to-all-start.10 = ((bf16[4,2,384,1024]{3,2,1,0:T(8,128)(2,1)}), bf16[4,2,384,1024]{3,2,1,0:T(8,128)(2,1)}, u32[]{:S(2)}, u32[]{:S(2)}) async-start(bf16[4,2,384,1024]{3,2,1,0:T(8,128)(2,1)} %copy.124), calls=%async_computation.10 | async-start | bytes 12582912 | tf_op jit(solution)/shard_map/all_to_all | solution.py:89
  (38 other events, 746.4 us)
Sparse Core Ops, SparseCore 0:
  652.8 321.6 reduce-scatter.14
  977.4 321.5 reduce-scatter.12
  1301.9 321.5 reduce-scatter.16
  1626.2 321.5 reduce-scatter.8
  1950.5 321.5 reduce-scatter.6
  2274.8 321.5 reduce-scatter.10
where the time goes:
time: 2610 us; the launch traced here: 2600 us
  waiting for transfers between devices  1260 us (48%)
  matrix products  783 us (30%)
  local copies, waits for them, and re-layouts  294 us (11%)
  other arithmetic  115 us (4%)
  blocking collectives  75.5 us (3%)
  starting transfers between devices  57.7 us (2%)
    reduce_scatter x6, waiting for transfers between devices, layer_backward(): lax.psum_scatter(grad_part, 'dp', scatter_dimension=1, tiled=True)  991 us
    all_to_all x6, waiting for transfers between devices, exchange(): return lax.all_to_all(shaped, 'ep', 0, 0)  147 us
    dot_general x2, matrix products, expert_backward(): jnp.einsum('secd,efd->escf', recv_dy, w_down, preferred_element_type=jnp....  138 us
    all_to_all x6, waiting for transfers between devices, give_back(): returned = lax.all_to_all(expert_rows, 'ep', 0, 0)  125 us
    dot_general x2, matrix products, expert_forward(): jnp.einsum('secd,edf->escf', recv_rows, w_up1, preferred_element_type=jnp...  76.2 us
    all_to_all x1, blocking collectives, exchange(): return lax.all_to_all(shaped, 'ep', 0, 0)  75.5 us
    gather x5, local copies, waits for them, and re-layouts, take_rows(): return jnp.take(values, row_tok, axis=0) * row_used[:, None]  69.4 us
    dot_general x2, matrix products, expert_backward(): jnp.einsum('secd,edf->escf', recv_rows, w_up1, preferred_element_type=jnp...  67.5 us
  transfers between devices with their start and end apart: 18, of which 12 were waited for; matrix products, arithmetic and copies ran while one was open for 35% of the time, Pallas kernels for 0%

commit v1 on v0

v1 whole, which is shorter than its diff:
```python
import jax
import jax.numpy as jnp
from jax import lax
from jax.sharding import PartitionSpec as P


F32 = jnp.float32
BF16 = jnp.bfloat16


def pair_slots(expert_ids, n_experts):
    n_tokens = expert_ids.shape[0]
    experts = jnp.arange(n_experts, dtype=jnp.int32)
    hit = expert_ids[:, :, None] == experts[None, None, :]
    count = jnp.any(hit, axis=1).astype(BF16)
    rows = lax.broadcasted_iota(jnp.int32, (n_tokens, n_tokens), 0)
    cols = lax.broadcasted_iota(jnp.int32, (n_tokens, n_tokens), 1)
    below = (cols < rows).astype(BF16)
    earlier = jnp.dot(below, count, preferred_element_type=F32).astype(jnp.int32)
    slot = jnp.sum(jnp.where(hit, earlier[:, None, :], 0), axis=2)
    return slot


def local_codes(expert_ids, slot, n_local, capacity, which):
    code = (expert_ids // n_local) * capacity + slot
    return jnp.where(expert_ids % n_local == which, code, -1)


def row_picker(code, n_rows):
    ids = lax.broadcasted_iota(jnp.int32, (n_rows, code.shape[0]), 0)
    picked = code[:, 0][None, :] == ids
    for j in range(1, code.shape[1]):
        picked = picked | (code[:, j][None, :] == ids)
    return picked.astype(BF16)


def token_picker(code_col, n_rows):
    ids = lax.broadcasted_iota(jnp.int32, (code_col.shape[0], n_rows), 1)
    return code_col[:, None] == ids


def place_gates(gate_vals, code, n_rows):
    ids = lax.broadcasted_iota(jnp.int32, (code.shape[0], n_rows), 1)
    total = jnp.zeros((code.shape[0], n_rows), F32)
    for j in range(code.shape[1]):
        total = total + jnp.where(code[:, j][:, None] == ids, gate_vals[:, j][:, None], 0.0)
    return jnp.sum(total, axis=0)


def solution(mesh):
    n_ep = mesh.shape['ep']
    n_dp = mesh.shape['dp']
    tok_spec = P(('pod', 'dp', 'ep'), None)
    weight_spec = P('ep', None, None)
    grad_spec = P(('pod', 'ep'), 'dp', None)
    assert n_dp == 2

    def local_step(x_start, route_a, route_b, gate_a, gate_b, grad_out, w1_a, w3_a, w2_a, w1_b, w3_b, w2_b):
        n_tokens, _ = x_start.shape
        top_k = route_a.shape[1]
        n_local, _, _ = w1_a.shape
        n_experts = n_local * n_ep
        capacity = 3 * n_tokens * top_k // (2 * n_experts)
        n_rows = n_ep * capacity
        dp = lax.axis_index('dp')

        def exchange(rows):
            shaped = rows.reshape((n_ep, capacity) + rows.shape[1:])
            return lax.all_to_all(shaped, 'ep', 0, 0).reshape(rows.shape)

        def dispatch(values, code):
            return jnp.dot(row_picker(code, n_rows), values, preferred_element_type=F32).astype(BF16)

        def plan(expert_ids):
            slot = pair_slots(expert_ids, n_experts)
            codes = [local_codes(expert_ids, slot, n_local, capacity, i) for i in range(n_local)]
            return codes, expert_ids * capacity + slot

        def expert_forward(rows, w_up1, w_up3, w_down):
            pre_one = jnp.dot(rows, w_up1, preferred_element_type=F32)
            pre_three = jnp.dot(rows, w_up3, preferred_element_type=F32)
            hidden = (jax.nn.silu(pre_one) * pre_three).astype(BF16)
            return jnp.dot(hidden, w_down, preferred_element_type=F32).astype(BF16)

        def mix_back(x_in, returned, codes, gate_vals):
            total = x_in.astype(F32)
            for rows, code in zip(returned, codes):
                for j in range(top_k):
                    picker = token_picker(code[:, j], n_rows).astype(BF16)
                    picked = jnp.dot(picker, rows, preferred_element_type=F32)
                    total = total + gate_vals[:, j][:, None] * picked
            return total.astype(BF16)

        def add_back(grad_in, returned, codes):
            total = grad_in.astype(F32)
            for i, code in enumerate(codes):
                picker = token_picker(code[:, 0], n_rows)
                for j in range(1, top_k):
                    picker = picker | token_picker(code[:, j], n_rows)
                total = total + jnp.dot(picker.astype(BF16), returned[i], preferred_element_type=F32)
            return total.astype(BF16)

        def gates_out(gate_vals, pair_row):
            placed = lax.optimization_barrier(place_gates(gate_vals, pair_row, n_experts * capacity))
            moved = lax.all_to_all(placed.reshape(n_ep, n_local * capacity), 'ep', 0, 0)
            moved = moved.reshape(n_ep, n_local, capacity)
            return [moved[:, i].reshape(n_rows) for i in range(n_local)]

        def gates_back(gate_grads, pair_row):
            joined = jnp.stack([grad.reshape(n_ep, capacity) for grad in gate_grads], axis=1)
            moved = lax.all_to_all(joined.reshape(n_ep, n_local * capacity), 'ep', 0, 0).reshape(-1)
            moved, pair_row = lax.optimization_barrier((moved, pair_row))
            cols = [jnp.sum(jnp.where(token_picker(pair_row[:, j], n_experts * capacity), moved[None, :], 0.0), axis=1)
                    for j in range(top_k)]
            return jnp.stack(cols, axis=1)

        def part(values, index):
            size = values.shape[1] // n_dp
            return lax.dynamic_slice_in_dim(values, index * size, size, axis=1)

        def grad_product(left, right):
            return lax.dot_general(left, right, (((0,), (0,)), ((), ())), preferred_element_type=F32)

        def to_peer(left, right):
            partial = grad_product(part(left, 1 - dp), right).astype(BF16)
            return lax.ppermute(partial, 'dp', [(0, 1), (1, 0)])

        def own_parts(lefts, rights, received):
            out = jnp.zeros((n_local, lefts[0].shape[1] // n_dp, rights[0].shape[1]), F32)
            for i in range(n_local):
                total = grad_product(part(lefts[i], dp), rights[i]) + received[i].astype(F32)
                out = lax.dynamic_update_slice(out, total[None], (i, 0, 0))
            return out

        def recompute(rows, w_up1, w_up3):
            pre_one = jnp.dot(rows, w_up1, preferred_element_type=F32)
            pre_three = jnp.dot(rows, w_up3, preferred_element_type=F32)
            hidden = (jax.nn.silu(pre_one) * pre_three).astype(BF16)
            return pre_one, pre_three, hidden

        def backward_inner(pre_one, pre_three, hidden, recv_dy, recv_gate, w_down):
            sig_one = jax.nn.sigmoid(pre_one)
            act_one = pre_one * sig_one
            back_proj = jnp.einsum('rd,fd->rf', recv_dy, w_down, preferred_element_type=F32)
            gate_grad = jnp.sum(back_proj * hidden.astype(F32), axis=-1)
            d_hidden = recv_gate[:, None] * back_proj
            d_one = (d_hidden * pre_three * sig_one * (1.0 + pre_one * (1.0 - sig_one))).astype(BF16)
            d_three = (d_hidden * act_one).astype(BF16)
            return gate_grad, d_one, d_three

        def row_grads(d_one, d_three, w_up1, w_up3):
            return (jnp.einsum('rf,df->rd', d_one, w_up1, preferred_element_type=F32)
                    + jnp.einsum('rf,df->rd', d_three, w_up3, preferred_element_type=F32)).astype(BF16)

        every = range(n_local)

        codes_a, pair_a = plan(route_a)
        codes_b, pair_b = plan(route_b)

        recv_a = [exchange(dispatch(x_start, codes_a[i])) for i in every]
        back_a = []
        for i in every:
            out_rows = expert_forward(recv_a[i], w1_a[i], w3_a[i], w2_a[i])
            back_a.append(exchange(out_rows))
        x_mid = mix_back(x_start, back_a, codes_a, gate_a)
        recv_b = [exchange(dispatch(x_mid, codes_b[i])) for i in every]

        x_kept, grad_kept = lax.optimization_barrier((x_start, grad_out))
        rows_b = [lax.optimization_barrier(rows) for rows in recv_b]

        def back_up(rows, grad_in, codes, pair_row, gate_vals, w_up1, w_up3, w_down):
            dy = [exchange(dispatch(grad_in, codes[i])) for i in every]
            gates = gates_out(gate_vals, pair_row)
            hid, pre, scaled, got2, gate_grads, d_one, d_three = [], [], [], [], [], [], []
            for i in every:
                one, three, hidden = recompute(rows[i], w_up1[i], w_up3[i])
                scaled.append((gates[i][:, None] * dy[i].astype(F32)).astype(BF16))
                one, three, hidden = lax.optimization_barrier((one, three, hidden))
                got2.append(to_peer(hidden, scaled[i]))
                hid.append(hidden)
                pre.append((one, three))
            for i in every:
                grad, one, three = backward_inner(pre[i][0], pre[i][1], hid[i], dy[i], gates[i], w_down[i])
                gate_grads.append(grad)
                d_one.append(one)
                d_three.append(three)
            got1 = [to_peer(rows[i], d_one[i]) for i in every]
            got3 = [to_peer(rows[i], d_three[i]) for i in every]
            returned = []
            for i in every:
                du_rows = row_grads(d_one[i], d_three[i], w_up1[i], w_up3[i])
                returned.append(exchange(du_rows))
            grad_x = add_back(grad_in, returned, codes)
            gate_out = gates_back(gate_grads, pair_row)

            def own():
                return (own_parts(rows, d_one, got1), own_parts(rows, d_three, got3),
                        own_parts(hid, scaled, got2))

            return grad_x, gate_out, own

        grad_mid, dgate_b, own_b = back_up(rows_b, grad_kept, codes_b, pair_b, gate_b, w1_b, w3_b, w2_b)
        rows_a = [exchange(dispatch(x_kept, codes_a[i])) for i in every]
        grad_x, dgate_a, own_a = back_up(rows_a, grad_mid, codes_a, pair_a, gate_a, w1_a, w3_a, w2_a)

        back_b = []
        for i in every:
            out_rows = expert_forward(recv_b[i], w1_b[i], w3_b[i], w2_b[i])
            back_b.append(exchange(out_rows))
        x_final = mix_back(x_mid, back_b, codes_b, gate_b)

        dw1_b, dw3_b, dw2_b = own_b()
        dw1_a, dw3_a, dw2_a = own_a()
        return (x_final, grad_x, dw1_a, dw3_a, dw2_a, dw1_b, dw3_b, dw2_b, dgate_a, dgate_b)

    return jax.shard_map(local_step, mesh=mesh,
                         in_specs=(tok_spec,) * 6 + (weight_spec,) * 6,
                         out_specs=(tok_spec, tok_spec) + (grad_spec,) * 6 + (tok_spec, tok_spec),
                         check_vma=False)
```

time: 2610 us -> 1810 us (0.69)
  waiting for transfers between devices: 1260 us -> 501 us
  matrix products: 783 us -> 1080 us
  local copies, waits for them, and re-layouts: 294 us -> 8.11 us
  blocking collectives: 75.5 us -> 0 us
  starting transfers between devices: 57.7 us -> 109 us
    reduce_scatter x6 -> x0, waiting for transfers between devices: 991 us -> none  [layer_backward(): lax.psum_scatter(grad_part, 'dp', scatter_dimension=1, tiled=True)]
    ppermute x0 -> x12, waiting for transfers between devices: none -> 338 us  [to_peer(): return lax.ppermute(partial, 'dp', [(0, 1), (1, 0)])]
    dot_general x22 -> x76, matrix products: 783 us -> 1080 us  [the longest x24 268 us: grad_product(): lax.dot_general(left, right, (((0,), (0,)), ((), ())), preferred_element_...]
    gather x11 -> x0, local copies, waits for them, and re-layouts: 151 us -> none  [the longest x5 69.4 us: take_rows(): return jnp.take(values, row_tok, axis=0) * row_used[:, None]]
    all_to_all x12 -> x22, waiting for transfers between devices: 272 us -> 162 us  [the longest x18 162 us: exchange(): return lax.all_to_all(shaped, 'ep', 0, 0).reshape(rows.shape)]
    all_to_all x1 -> x0, blocking collectives: 75.5 us -> none  [exchange(): return lax.all_to_all(shaped, 'ep', 0, 0)]
    dynamic_update_slice x0 -> x6, other arithmetic: none -> 74.4 us  [own_parts(): out = lax.dynamic_update_slice(out, total[None], (i, 0, 0))]
    convert_element_type x8 -> x0, local copies, waits for them, and re-layouts: 67 us -> none  [the longest x2 21.2 us: mix_back(): mixed_sum = jnp.sum(gate_vals[:, :, None] * pair_out, axis=1)]
  transfers between devices with their start and end apart: 18 -> 34, of which waited for: 12 -> 17; matrix products, arithmetic and copies ran while one was open for 35% -> 63% of each run, Pallas kernels for 0% -> 0%
where the time goes in v1:
time: 1810 us; the launch traced here: 1800 us
  matrix products  1080 us (60%)
  waiting for transfers between devices  501 us (28%)
  starting transfers between devices  109 us (6%)
  other arithmetic  100 us (6%)
    ppermute x12, waiting for transfers between devices, to_peer(): return lax.ppermute(partial, 'dp', [(0, 1), (1, 0)])  338 us
    dot_general x24, matrix products, grad_product(): lax.dot_general(left, right, (((0,), (0,)), ((), ())), preferred_element_...  268 us
    all_to_all x18, waiting for transfers between devices, exchange(): return lax.all_to_all(shaped, 'ep', 0, 0).reshape(rows.shape)  162 us
    dot_general x4, matrix products, backward_inner(): jnp.einsum('rd,fd->rf', recv_dy, w_down, preferred_element_type=F32)  148 us
    dot_general x4, matrix products, expert_forward(): return jnp.dot(hidden, w_down, preferred_element_type=F32).astype(BF16)  128 us
    dot_general x4, matrix products, recompute(): pre_three = jnp.dot(rows, w_up3, preferred_element_type=F32)  106 us
    all_to_all x18, starting transfers between devices, exchange(): return lax.all_to_all(shaped, 'ep', 0, 0).reshape(rows.shape)  81.9 us
    dynamic_update_slice x6, other arithmetic, own_parts(): out = lax.dynamic_update_slice(out, total[None], (i, 0, 0))  74.4 us
  transfers between devices with their start and end apart: 34, of which 17 were waited for; matrix products, arithmetic and copies ran while one was open for 63% of the time, Pallas kernels for 0%

profile of v1, /device:TPU:0, one launch (start us, length us, event | category | flops | bytes accessed | tf_op | source)
XLA Modules:
  0.0 1797.6 jit_solution(12815379732329665768)
XLA Ops:
  65.1 20.6 %all-to-all-done.2 = bf16[4,384,1024]{2,1,0:T(8,128)(2,1)S(1)} async-done(((bf16[4,384,1024]{2,1,0:T(8,128)(2,1)}), bf16[4,384,1024]{2,1,0:T(8,128)(2,1)S(1)}, u32[]{:S(2)}, u32[]{:S(2)}) %all-to-all-start.2) | async-done | bytes 3145760 | tf_op jit(solution)/shard_map/all_to_all | solution.py:69
  131.4 32.0 %fusion.180 = bf16[1536,1024]{1,0:T(8,128)(2,1)} fusion(bf16[2,3584,1024]{2,1,0:T(8,128)(2,1)} %param.20, f32[1536,3584]{1,0:T(8,128)} %fusion.51, bf16[1536,1024]{1,0:T(8,128)(2,1)} %bitcast.304, bf16[2,1024,3584]{2,1,0:T(8,128)(2,1)} %param.19), kind=kOutput, calls=%fused_computation.233 | convolution fusion | flops 22583181312 | bytes 42991616 | tf_op jit(solution)/shard_map/dot_general | solution.py:83
  163.5 19.1 %fusion.66 = f32[1536,3584]{1,0:T(8,128)} fusion(bf16[1536,1024]{1,0:T(8,128)(2,1)} %bitcast.4, bf16[2,1024,3584]{2,1,0:T(8,128)(2,1)} %param.18), kind=kOutput, calls=%fused_computation.106 | convolution fusion | flops 11274289152 | bytes 32505856 | tf_op jit(solution)/shard_map/dot_general | solution.py:80
  188.1 32.0 %fusion.185 = bf16[1536,1024]{1,0:T(8,128)(2,1)} fusion(bf16[2,3584,1024]{2,1,0:T(8,128)(2,1)} %param.20, f32[1536,3584]{1,0:T(8,128)} %fusion.66, bf16[1536,1024]{1,0:T(8,128)(2,1)} %bitcast.4, bf16[2,1024,3584]{2,1,0:T(8,128)(2,1)} %param.19), kind=kOutput, calls=%fused_computation.234 | convolution fusion | flops 22583181312 | bytes 42991616 | tf_op jit(solution)/shard_map/dot_general | solution.py:83
  220.2 18.9 %fusion.64 = f32[1536,3584]{1,0:T(8,128)} fusion(bf16[1536,1024]{1,0:T(8,128)(2,1)} %bitcast.282, bf16[2,1024,3584]{2,1,0:T(8,128)(2,1)} %param.18), kind=kOutput, calls=%fused_computation.104 | convolution fusion | flops 11274289152 | bytes 32505856 | tf_op jit(solution)/shard_map/dot_general | solution.py:136
  243.8 27.3 %multiply_convert_fusion.5 = (bf16[1536,3584]{1,0:T(8,128)(2,1)}, f32[1536,3584]{1,0:T(8,128)}) fusion(f32[1536,3584]{1,0:T(8,128)} %fusion.64, bf16[1536,1024]{1,0:T(8,128)(2,1)} %bitcast.283, bf16[2,1024,3584]{2,1,0:T(8,128)(2,1)} %param.19), kind=kOutput, calls=%fused_computation.11 | convolution fusion | flops 11307319296 | bytes 65536000 | tf_op jit(solution)/shard_map/dot_general | solution.py:137
  345.0 25.7 %multiply_convert_fusion.2 = (bf16[1536,3584]{1,0:T(8,128)(2,1)}, f32[1536,3584]{1,0:T(8,128)}) fusion(f32[1536,3584]{1,0:T(8,128)} %fusion.49, bf16[1536,1024]{1,0:T(8,128)(2,1)S(1)} %bitcast.277, bf16[2,1024,3584]{2,1,0:T(8,128)(2,1)} %param.19), kind=kOutput, calls=%fused_computation.7 | convolution fusion | flops 11307319296 | bytes 65536000 | tf_op jit(solution)/shard_map/dot_general | solution.py:137
  385.8 19.1 %fusion.21 = f32[1536,3584]{1,0:T(8,128)} fusion(bf16[1536,1024]{1,0:T(8,128)(2,1)} %bitcast.34, bf16[2,1024,3584]{2,1,0:T(8,128)(2,1)} %param.21), kind=kOutput, calls=%fused_computation.64 | convolution fusion | flops 11274289152 | bytes 32505856 | tf_op jit(solution)/shard_map/dot_general | solution.py:80
  446.6 31.7 %fusion.175 = bf16[1536,1024]{1,0:T(8,128)(2,1)} fusion(bf16[2,3584,1024]{2,1,0:T(8,128)(2,1)} %param.23, f32[1536,3584]{1,0:T(8,128)} %fusion.36, bf16[1536,1024]{1,0:T(8,128)(2,1)S(1)} %bitcast.289, bf16[2,1024,3584]{2,1,0:T(8,128)(2,1)} %param.22), kind=kOutput, calls=%fused_computation.232 | convolution fusion | flops 22583181312 | bytes 42991616 | tf_op jit(solution)/shard_map/dot_general | solution.py:83
  478.3 32.5 %fusion.170 = bf16[1536,1024]{1,0:T(8,128)(2,1)} fusion(bf16[2,3584,1024]{2,1,0:T(8,128)(2,1)} %param.23, f32[1536,3584]{1,0:T(8,128)} %fusion.21, bf16[1536,1024]{1,0:T(8,128)(2,1)} %bitcast.34, bf16[2,1024,3584]{2,1,0:T(8,128)(2,1)} %param.22), kind=kOutput, calls=%fused_computation.231 | convolution fusion | flops 22583181312 | bytes 42991616 | tf_op jit(solution)/shard_map/dot_general | solution.py:83
  510.8 27.2 %multiply_convert_fusion.8 = (bf16[1536,3584]{1,0:T(8,128)(2,1)}, f32[1536,3584]{1,0:T(8,128)}) fusion(f32[1536,3584]{1,0:T(8,128)} %fusion.19, bf16[1536,1024]{1,0:T(8,128)(2,1)} %bitcast.34, bf16[2,1024,3584]{2,1,0:T(8,128)(2,1)} %param.22), kind=kOutput, calls=%fused_computation.15 | convolution fusion | flops 11307319296 | bytes 65536000 | tf_op jit(solution)/shard_map/dot_general | solution.py:137
  561.1 37.0 %multiply_convert_fusion.7 = (bf16[1536,3584]{1,0:T(8,128)(2,1)}, bf16[1536,3584]{1,0:T(8,128)(2,1)}, f32[1536]{0:T(1024)S(1)}) fusion(f32[1536,3584]{1,0:T(8,128)} %fusion.19, f32[1536,3584]{1,0:T(8,128)} %get-tuple-element.31, f32[1536]{0:T(1024)S(1)} %copy-done.22, bf16[1536,3584]{1,0:T(8,128)(2,1)} %get-tuple-element.41, ...), kind=kOutput, calls=%fused_computation.13 | convolution fusion | flops 11367872512 | bytes 87568384 | tf_op jit(solution)/shard_map/rd,fd->rf/dot_general | solution.py:144
  632.1 25.8 %multiply_convert_fusion.11 = (bf16[1536,3584]{1,0:T(8,128)(2,1)}, f32[1536,3584]{1,0:T(8,128)}) fusion(f32[1536,3584]{1,0:T(8,128)} %fusion.34, bf16[1536,1024]{1,0:T(8,128)(2,1)S(1)} %bitcast.291, bf16[2,1024,3584]{2,1,0:T(8,128)(2,1)} %param.22), kind=kOutput, calls=%fused_computation.19 | convolution fusion | flops 11307319296 | bytes 65536000 | tf_op jit(solution)/shard_map/dot_general | solution.py:137
  668.3 37.0 %multiply_convert_fusion.10 = (bf16[1536,3584]{1,0:T(8,128)(2,1)}, bf16[1536,3584]{1,0:T(8,128)(2,1)}, f32[1536]{0:T(1024)S(1)}) fusion(f32[1536,3584]{1,0:T(8,128)} %fusion.34, f32[1536,3584]{1,0:T(8,128)} %get-tuple-element.29, f32[1536]{0:T(1024)S(1)} %copy-done.20, bf16[1536,3584]{1,0:T(8,128)(2,1)} %get-tuple-element.40, ...), kind=kOutput, calls=%fused_computation.17 | convolution fusion | flops 11367872512 | bytes 87568384 | tf_op jit(solution)/shard_map/rd,fd->rf/dot_general | solution.py:144
  790.9 19.4 %all-to-all-done.7 = bf16[4,384,1024]{2,1,0:T(8,128)(2,1)S(1)} async-done(((bf16[4,384,1024]{2,1,0:T(8,128)(2,1)}), bf16[4,384,1024]{2,1,0:T(8,128)(2,1)S(1)}, u32[]{:S(2)}, u32[]{:S(2)}) %all-to-all-start.7) | async-done | bytes 3145760 | tf_op jit(solution)/shard_map/all_to_all | solution.py:69
  873.4 20.1 %all-to-all-done.12 = bf16[4,384,1024]{2,1,0:T(8,128)(2,1)} async-done(((bf16[4,384,1024]{2,1,0:T(8,128)(2,1)}), bf16[4,384,1024]{2,1,0:T(8,128)(2,1)}, u32[]{:S(2)}, u32[]{:S(2)}) %all-to-all-start.12) | async-done | bytes 3145760 | tf_op jit(solution)/shard_map/all_to_all | solution.py:69
  915.6 20.0 %all-to-all-done.5 = bf16[4,384,1024]{2,1,0:T(8,128)(2,1)} async-done(((bf16[4,384,1024]{2,1,0:T(8,128)(2,1)}), bf16[4,384,1024]{2,1,0:T(8,128)(2,1)}, u32[]{:S(2)}, u32[]{:S(2)}) %all-to-all-start.5) | async-done | bytes 3145760 | tf_op jit(solution)/shard_map/all_to_all | solution.py:69
  1061.2 42.4 %collective-permute-done.6 = bf16[512,3584]{1,0:T(8,128)(2,1)} collective-permute-done((bf16[512,3584]{1,0:T(8,128)(2,1)}, bf16[512,3584]{1,0:T(8,128)(2,1)}, u32[]{:S(2)}, u32[]{:S(2)}) %collective-permute-start.6) | collective-permute-done | bytes 3670048 | tf_op jit(solution)/shard_map/ppermute | solution.py:126
  1143.5 37.1 %multiply_convert_fusion.4 = (bf16[1536,3584]{1,0:T(8,128)(2,1)}, bf16[1536,3584]{1,0:T(8,128)(2,1)}, f32[1536]{0:T(1024)S(1)}) fusion(f32[1536,3584]{1,0:T(8,128)} %fusion.64, f32[1536,3584]{1,0:T(8,128)} %get-tuple-element.34, f32[1536]{0:T(1024)S(1)} %copy-done.18, bf16[1536,3584]{1,0:T(8,128)(2,1)} %get-tuple-element.38, ...), kind=kOutput, calls=%fused_computation.9 | convolution fusion | flops 11367872512 | bytes 87568384 | tf_op jit(solution)/shard_map/rd,fd->rf/dot_general | solution.py:144
  1250.4 37.1 %multiply_convert_fusion.1 = (bf16[1536,3584]{1,0:T(8,128)(2,1)}, bf16[1536,3584]{1,0:T(8,128)(2,1)}, f32[1536]{0:T(1024)S(1)}) fusion(f32[1536,3584]{1,0:T(8,128)} %fusion.49, f32[1536,3584]{1,0:T(8,128)} %get-tuple-element.36, f32[1536]{0:T(1024)S(1)} %copy-done.17, bf16[1536,3584]{1,0:T(8,128)(2,1)} %get-tuple-element.39, ...), kind=kOutput, calls=%fused_computation.5 | convolution fusion | flops 11367872512 | bytes 87568384 | tf_op jit(solution)/shard_map/rd,fd->rf/dot_general | solution.py:144
  1421.7 114.7 %collective-permute-done = bf16[512,3584]{1,0:T(8,128)(2,1)} collective-permute-done((bf16[512,3584]{1,0:T(8,128)(2,1)}, bf16[512,3584]{1,0:T(8,128)(2,1)}, u32[]{:S(2)}, u32[]{:S(2)}) %collective-permute-start) | collective-permute-done | bytes 3670048 | tf_op jit(solution)/shard_map/ppermute | solution.py:126
  1546.5 68.5 %collective-permute-done.3 = bf16[512,3584]{1,0:T(8,128)(2,1)} collective-permute-done((bf16[512,3584]{1,0:T(8,128)(2,1)}, bf16[512,3584]{1,0:T(8,128)(2,1)}, u32[]{:S(2)}, u32[]{:S(2)}) %collective-permute-start.3) | collective-permute-done | bytes 3670048 | tf_op jit(solution)/shard_map/ppermute | solution.py:126
  1627.7 66.0 %collective-permute-done.1 = bf16[512,3584]{1,0:T(8,128)(2,1)} collective-permute-done((bf16[512,3584]{1,0:T(8,128)(2,1)}, bf16[512,3584]{1,0:T(8,128)(2,1)}, u32[]{:S(2)}, u32[]{:S(2)}) %collective-permute-start.1) | collective-permute-done | bytes 3670048 | tf_op jit(solution)/shard_map/ppermute | solution.py:126
  1738.4 33.4 %collective-permute-done.5 = bf16[1792,1024]{1,0:T(8,128)(2,1)} collective-permute-done((bf16[1792,1024]{1,0:T(8,128)(2,1)}, bf16[1792,1024]{1,0:T(8,128)(2,1)}, u32[]{:S(2)}, u32[]{:S(2)}) %collective-permute-start.5) | collective-permute-done | bytes 3670048 | tf_op jit(solution)/shard_map/ppermute | solution.py:126
  (334 shorter events, 950.6 us)
Async XLA Ops:
  127.3 55.2 %all-to-all-start.15 = ((bf16[4,384,1024]{2,1,0:T(8,128)(2,1)}), bf16[4,384,1024]{2,1,0:T(8,128)(2,1)S(1)}, u32[]{:S(2)}, u32[]{:S(2)}) async-start(bf16[4,384,1024]{2,1,0:T(8,128)(2,1)} %bitcast.302), calls=%async_computation.15 | async-start | bytes 6291456 | tf_op jit(solution)/shard_map/all_to_all | solution.py:69
  184.2 54.8 %all-to-all-start.18 = ((bf16[4,384,1024]{2,1,0:T(8,128)(2,1)}), bf16[4,384,1024]{2,1,0:T(8,128)(2,1)S(1)}, u32[]{:S(2)}, u32[]{:S(2)}) async-start(bf16[4,384,1024]{2,1,0:T(8,128)(2,1)} %bitcast.307), calls=%async_computation.18 | async-start | bytes 6291456 | tf_op jit(solution)/shard_map/all_to_all | solution.py:69
  239.1 41.6 %all-to-all-start.3 = ((bf16[4,384,1024]{2,1,0:T(8,128)(2,1)}), bf16[4,384,1024]{2,1,0:T(8,128)(2,1)}, u32[]{:S(2)}, u32[]{:S(2)}) async-start(bf16[4,384,1024]{2,1,0:T(8,128)(2,1)} %bitcast.313), calls=%async_computation.3 | async-start | bytes 6291456 | tf_op jit(solution)/shard_map/all_to_all | solution.py:69
  280.7 41.8 %all-to-all-start.1 = ((bf16[4,384,1024]{2,1,0:T(8,128)(2,1)}), bf16[4,384,1024]{2,1,0:T(8,128)(2,1)}, u32[]{:S(2)}, u32[]{:S(2)}) async-start(bf16[4,384,1024]{2,1,0:T(8,128)(2,1)} %bitcast.314), calls=%async_computation.1 | async-start | bytes 6291456 | tf_op jit(solution)/shard_map/all_to_all | solution.py:69
  381.9 41.9 %all-to-all-start.4 = ((bf16[4,384,1024]{2,1,0:T(8,128)(2,1)}), bf16[4,384,1024]{2,1,0:T(8,128)(2,1)S(1)}, u32[]{:S(2)}, u32[]{:S(2)}) async-start(bf16[4,384,1024]{2,1,0:T(8,128)(2,1)} %bitcast.316), calls=%async_computation.4 | async-start | bytes 6291456 | tf_op jit(solution)/shard_map/all_to_all | solution.py:69
  423.8 132.3 %all-to-all-start.11 = ((bf16[4,384,1024]{2,1,0:T(8,128)(2,1)}), bf16[4,384,1024]{2,1,0:T(8,128)(2,1)}, u32[]{:S(2)}, u32[]{:S(2)}) async-start(bf16[4,384,1024]{2,1,0:T(8,128)(2,1)} %bitcast.301), calls=%async_computation.11 | async-start | bytes 6291456 | tf_op jit(solution)/shard_map/all_to_all | solution.py:69
  556.2 101.8 %all-to-all-start.9 = ((bf16[4,384,1024]{2,1,0:T(8,128)(2,1)}), bf16[4,384,1024]{2,1,0:T(8,128)(2,1)}, u32[]{:S(2)}, u32[]{:S(2)}) async-start(bf16[4,384,1024]{2,1,0:T(8,128)(2,1)} %bitcast.300), calls=%async_computation.9 | async-start | bytes 6291456 | tf_op jit(solution)/shard_map/all_to_all | solution.py:69
  628.1 335.3 %collective-permute-start.11 = (bf16[1792,1024]{1,0:T(8,128)(2,1)}, bf16[1792,1024]{1,0:T(8,128)(2,1)}, u32[]{:S(2)}, u32[]{:S(2)}) collective-permute-start(bf16[1792,1024]{1,0:T(8,128)(2,1)} %fusion.199), channel_id=1, source_target_pairs={{0,4},{4,0},{1,5},{5,1},{2,6},{6,2},{3,7},{7,3}} | collective-permute-start | bytes 11010056 | tf_op jit(solution)/shard_map/ppermute | solution.py:126
  630.0 369.9 %collective-permute-start.9 = (bf16[512,3584]{1,0:T(8,128)(2,1)}, bf16[512,3584]{1,0:T(8,128)(2,1)}, u32[]{:S(2)}, u32[]{:S(2)}) collective-permute-start(bf16[512,3584]{1,0:T(8,128)(2,1)} %convolution_convert_fusion), channel_id=1, source_target_pairs={{0,4},{4,0},{1,5},{5,1},{2,6},{6,2},{3,7},{7,3}} | collective-permute-start | bytes 11010056 | tf_op jit(solution)/shard_map/ppermute | solution.py:126
  630.1 419.5 %collective-permute-start.7 = (bf16[512,3584]{1,0:T(8,128)(2,1)}, bf16[512,3584]{1,0:T(8,128)(2,1)}, u32[]{:S(2)}, u32[]{:S(2)}) collective-permute-start(bf16[512,3584]{1,0:T(8,128)(2,1)} %convolution_convert_fusion.2), channel_id=1, source_target_pairs={{0,4},{4,0},{1,5},{5,1},{2,6},{6,2},{3,7},{7,3}} | collective-permute-start | bytes 11010056 | tf_op jit(solution)/shard_map/ppermute | solution.py:126
  706.0 63.7 %all-to-all-start.21 = ((f32[4,1,768]{2,1,0:T(1,128)}), f32[4,1,768]{2,1,0:T(1,128)S(1)}, u32[]{:S(2)}, u32[]{:S(2)}) async-start(f32[4,1,768]{2,1,0:T(1,128)} %all_to_all.102), calls=%async_computation.21 | async-start | bytes 24576 | tf_op jit(solution)/shard_map/all_to_all | solution.py:111
  767.7 207.5 %collective-permute-start.10 = (bf16[1792,1024]{1,0:T(8,128)(2,1)}, bf16[1792,1024]{1,0:T(8,128)(2,1)}, u32[]{:S(2)}, u32[]{:S(2)}) collective-permute-start(bf16[1792,1024]{1,0:T(8,128)(2,1)} %fusion.196), channel_id=1, source_target_pairs={{0,4},{4,0},{1,5},{5,1},{2,6},{6,2},{3,7},{7,3}} | collective-permute-start | bytes 11010056 | tf_op jit(solution)/shard_map/ppermute | solution.py:126
  767.7 257.5 %collective-permute-start.8 = (bf16[512,3584]{1,0:T(8,128)(2,1)}, bf16[512,3584]{1,0:T(8,128)(2,1)}, u32[]{:S(2)}, u32[]{:S(2)}) collective-permute-start(bf16[512,3584]{1,0:T(8,128)(2,1)} %convolution_convert_fusion.1), channel_id=1, source_target_pairs={{0,4},{4,0},{1,5},{5,1},{2,6},{6,2},{3,7},{7,3}} | collective-permute-start | bytes 11010056 | tf_op jit(solution)/shard_map/ppermute | solution.py:126
  893.5 42.0 %all-to-all-start.5 = ((bf16[4,384,1024]{2,1,0:T(8,128)(2,1)}), bf16[4,384,1024]{2,1,0:T(8,128)(2,1)}, u32[]{:S(2)}, u32[]{:S(2)}) async-start(bf16[4,384,1024]{2,1,0:T(8,128)(2,1)} %bitcast.28), calls=%async_computation.5 | async-start | bytes 6291456 | tf_op jit(solution)/shard_map/all_to_all | solution.py:69
  947.5 180.8 %all-to-all-start.14 = ((bf16[4,384,1024]{2,1,0:T(8,128)(2,1)}), bf16[4,384,1024]{2,1,0:T(8,128)(2,1)}, u32[]{:S(2)}, u32[]{:S(2)}) async-start(bf16[4,384,1024]{2,1,0:T(8,128)(2,1)} %bitcast.54), calls=%async_computation.14 | async-start | bytes 6291456 | tf_op jit(solution)/shard_map/all_to_all | solution.py:69
  963.5 140.1 %collective-permute-start.6 = (bf16[512,3584]{1,0:T(8,128)(2,1)}, bf16[512,3584]{1,0:T(8,128)(2,1)}, u32[]{:S(2)}, u32[]{:S(2)}) collective-permute-start(bf16[512,3584]{1,0:T(8,128)(2,1)} %convolution_convert_fusion.3), channel_id=1, source_target_pairs={{0,4},{4,0},{1,5},{5,1},{2,6},{6,2},{3,7},{7,3}} | collective-permute-start | bytes 11010056 | tf_op jit(solution)/shard_map/ppermute | solution.py:126
  1128.3 111.5 %all-to-all-start.17 = ((bf16[4,384,1024]{2,1,0:T(8,128)(2,1)}), bf16[4,384,1024]{2,1,0:T(8,128)(2,1)}, u32[]{:S(2)}, u32[]{:S(2)}) async-start(bf16[4,384,1024]{2,1,0:T(8,128)(2,1)} %bitcast.60), calls=%async_computation.17 | async-start | bytes 6291456 | tf_op jit(solution)/shard_map/all_to_all | solution.py:69
  1220.9 187.7 %collective-permute-start.2 = (bf16[512,3584]{1,0:T(8,128)(2,1)}, bf16[512,3584]{1,0:T(8,128)(2,1)}, u32[]{:S(2)}, u32[]{:S(2)}) collective-permute-start(bf16[512,3584]{1,0:T(8,128)(2,1)} %convolution_convert_fusion.5), channel_id=1, source_target_pairs={{0,4},{4,0},{1,5},{5,1},{2,6},{6,2},{3,7},{7,3}} | collective-permute-start | bytes 11010056 | tf_op jit(solution)/shard_map/ppermute | solution.py:126
  1358.8 41.8 %all-to-all-start.19 = ((bf16[4,384,1024]{2,1,0:T(8,128)(2,1)}), bf16[4,384,1024]{2,1,0:T(8,128)(2,1)}, u32[]{:S(2)}, u32[]{:S(2)}) async-start(bf16[4,384,1024]{2,1,0:T(8,128)(2,1)} %bitcast.310), calls=%async_computation.19 | async-start | bytes 6291456 | tf_op jit(solution)/shard_map/all_to_all | solution.py:69
  1375.2 351.5 %collective-permute-start.4 = (bf16[1792,1024]{1,0:T(8,128)(2,1)}, bf16[1792,1024]{1,0:T(8,128)(2,1)}, u32[]{:S(2)}, u32[]{:S(2)}) collective-permute-start(bf16[1792,1024]{1,0:T(8,128)(2,1)} %fusion.190), channel_id=1, source_target_pairs={{0,4},{4,0},{1,5},{5,1},{2,6},{6,2},{3,7},{7,3}} | collective-permute-start | bytes 11010056 | tf_op jit(solution)/shard_map/ppermute | solution.py:126
  1375.4 160.9 %collective-permute-start = (bf16[512,3584]{1,0:T(8,128)(2,1)}, bf16[512,3584]{1,0:T(8,128)(2,1)}, u32[]{:S(2)}, u32[]{:S(2)}) collective-permute-start(bf16[512,3584]{1,0:T(8,128)(2,1)} %convolution_convert_fusion.7), channel_id=1, source_target_pairs={{0,4},{4,0},{1,5},{5,1},{2,6},{6,2},{3,7},{7,3}} | collective-permute-start | bytes 11010056 | tf_op jit(solution)/shard_map/ppermute | solution.py:126
  1377.2 237.8 %collective-permute-start.3 = (bf16[512,3584]{1,0:T(8,128)(2,1)}, bf16[512,3584]{1,0:T(8,128)(2,1)}, u32[]{:S(2)}, u32[]{:S(2)}) collective-permute-start(bf16[512,3584]{1,0:T(8,128)(2,1)} %convolution_convert_fusion.4), channel_id=1, source_target_pairs={{0,4},{4,0},{1,5},{5,1},{2,6},{6,2},{3,7},{7,3}} | collective-permute-start | bytes 11010056 | tf_op jit(solution)/shard_map/ppermute | solution.py:126
  1377.4 316.2 %collective-permute-start.1 = (bf16[512,3584]{1,0:T(8,128)(2,1)}, bf16[512,3584]{1,0:T(8,128)(2,1)}, u32[]{:S(2)}, u32[]{:S(2)}) collective-permute-start(bf16[512,3584]{1,0:T(8,128)(2,1)} %convolution_convert_fusion.6), channel_id=1, source_target_pairs={{0,4},{4,0},{1,5},{5,1},{2,6},{6,2},{3,7},{7,3}} | collective-permute-start | bytes 11010056 | tf_op jit(solution)/shard_map/ppermute | solution.py:126
  1408.6 363.2 %collective-permute-start.5 = (bf16[1792,1024]{1,0:T(8,128)(2,1)}, bf16[1792,1024]{1,0:T(8,128)(2,1)}, u32[]{:S(2)}, u32[]{:S(2)}) collective-permute-start(bf16[1792,1024]{1,0:T(8,128)(2,1)} %fusion.193), channel_id=1, source_target_pairs={{0,4},{4,0},{1,5},{5,1},{2,6},{6,2},{3,7},{7,3}} | collective-permute-start | bytes 11010056 | tf_op jit(solution)/shard_map/ppermute | solution.py:126
  (92 other events, 2622.5 us)
